TPU v7x, 128 devices: a whole 4x4x4 slice. The times are simulated.
128 devices in a mesh: sector: 16 (over z_lo, y, core), op: 8 (over x, z_hi).
Axes of the slice: x: 4, y: 4, z: 4 (z_hi: 2, z_lo: 2; z = z_hi * 2 + z_lo), core: 2. Of those that a mesh axis runs over, the one named last changes fastest.
Arguments:
- wavefunction: bfloat16 [16, 768, 1536], P('sector', 'op'), may hold values from -6 to 6
- basis: bfloat16 [16, 1536, 768], P('sector'), may hold values from -0.15625 to 0.15625
- left_ops: bfloat16 [40, 768, 768], P('op'), may hold values from -0.03125 to 0.03125
- right_ops: bfloat16 [40, 768, 768], P('op'), may hold values from -0.21875 to 0.21875
- offsets: int32 [40], P('op'), may hold values from -2 to 2, as said below
- sector_sizes: int32 [16], P('sector'), may hold values from 384 to 1536
Outputs:
- evolved: bfloat16 [16, 768, 1536], P('sector', 'op')
Inputs may be any that keep to these rules, and one draw needn't show every extreme that they name: Every value from -2 to 2 occurs among the 40 offsets, any two of them equally often up to one. Only the first sector_sizes[s] left states of sector s are live.
All inputs are finite; a program needn't handle non-finite values.
Results may differ from a plain program's by a relative error of at most 0.014.
Values may be sent and summed in bfloat16 or wider, within the bound.
A program may use at most 128 MiB of HBM per device.

v0:
```python
import jax
import jax.numpy as jnp
from jax import lax
from jax.sharding import PartitionSpec as P

REACH = 2
STEPS = 2


increment_width = 0.75


def laid_out(parts, dim):
    parts = jnp.moveaxis(parts, 0, dim)
    lengths = parts.shape
    return parts.reshape(*lengths[:dim], lengths[dim] * lengths[dim + 1], *lengths[dim + 2 :])


def sent_to_all(array, axis):
    copies = jnp.broadcast_to(array, (lax.axis_size(axis), *array.shape))
    return lax.all_to_all(copies, axis, split_axis=0, concat_axis=0, tiled=True)


def gathered_copies(array, axis, dim):
    return laid_out(sent_to_all(array, axis), dim)


def from_behind(array, axis, by):
    peers = lax.axis_size(axis)
    pairs = [(i, i + by) for i in range(peers) if 0 <= i + by < peers]
    return lax.ppermute(array, axis, pairs)


def split_up(array, dim, peers):
    before, after = (array.shape[:dim], array.shape[dim + 1 :])
    return jnp.moveaxis(array.reshape(*before, peers, -1, *after), dim, 0)


def summed_on_arrival(array, axis, dim):
    parts = split_up(array, dim, lax.axis_size(axis))
    arrived = lax.all_to_all(parts, axis, split_axis=0, concat_axis=0, tiled=True)
    return arrived.astype(jnp.float32).sum(axis=0)


def on_device(wavefunction, basis, left_ops, right_ops, offsets, sector_sizes):
    active_lines = sector_sizes[0]
    column_entries = lax.broadcasted_iota(jnp.int32, wavefunction.shape, 2)
    current = jnp.where(column_entries < active_lines, wavefunction, jnp.zeros_like(wavefunction))[
        0
    ]
    basis_index = lax.broadcasted_iota(jnp.int32, basis.shape, 1)
    masked_basis = jnp.where(basis_index < active_lines, basis, jnp.zeros_like(basis))[0]
    deltas = lax.broadcasted_iota(jnp.int32, (offsets.shape[0], 2 * REACH + 1), 1) - REACH
    picker = (offsets[:, None] == deltas).astype(jnp.bfloat16)
    for repeat in range(STEPS):
        transformed_blocks = jnp.dot(
            current, masked_basis, preferred_element_type=jnp.float32
        ).astype(jnp.bfloat16)
        gathered = gathered_copies(transformed_blocks, "op", 0)
        blocks = []
        for offset in range(-REACH, REACH + 1):
            if offset == 0:
                blocks.append(gathered)
            else:
                blocks.append(from_behind(gathered, "sector", -offset))
        candidates = jnp.stack(blocks)
        selected = jnp.einsum(
            "kd,dij->kij", picker, candidates, preferred_element_type=jnp.float32
        ).astype(jnp.bfloat16)
        half_product = jnp.einsum(
            "kab,kbc->kac", left_ops, selected, preferred_element_type=jnp.float32
        ).astype(jnp.bfloat16)
        overall_tile_count = summed_on_arrival(
            jnp.einsum(
                "kac,kdc->ad", half_product, right_ops, preferred_element_type=jnp.float32
            ).astype(jnp.bfloat16),
            "op",
            0,
        ).astype(jnp.bfloat16)
        lifted_tiles = jnp.einsum(
            "ad,ld->al", overall_tile_count, masked_basis, preferred_element_type=jnp.float32
        )
        current = (current.astype(jnp.float32) - increment_width * lifted_tiles).astype(
            jnp.bfloat16
        )
    return current[None]


def solution(mesh):
    return jax.shard_map(
        on_device,
        mesh=mesh,
        in_specs=(
            P("sector", "op", None),
            P("sector", None, None),
            P("op", None, None),
            P("op", None, None),
            P("op"),
            P("sector"),
        ),
        out_specs=P("sector", "op", None),
        check_vma=False,
    )
```

profile of v0, /device:TPU:9, one launch (start us, length us, event | category | flops | bytes accessed | tf_op | source)
XLA Modules:
  0.0 266.7 jit_solution(13425826634388701599)
XLA Ops:
  0.7 2.5 fusion.33
  3.2 24.3 %all_to_all.20 = bf16[8,96,768]{2,1,0:T(8,128)(2,1)S(1)} all-to-all(bf16[8,96,768]{2,1,0:T(8,128)(2,1)S(1)} %broadcast_in_dim.18), channel_id=1, replica_groups=mesh['sector'=16,'op'=8] {'op'}, dimensions={0} | all-to-all | bytes 2359296 | tf_op jit(solution)/shard_map/all_to_all | solution.py:21
  27.5 3.2 %collective-permute-start = (bf16[768,768]{1,0:T(8,128)(2,1)S(1)}, bf16[768,768]{1,0:T(8,128)(2,1)S(1)}, u32[]{:S(2)}, u32[]{:S(2)}) collective-permute-start(bf16[768,768]{1,0:T(8,128)(2,1)S(1)} %bitcast.79), channel_id=1, source_target_pairs={{0,16},{8,24},{16,32},{24,40},{32,48},{40,56},{48,64},{56,72},{64,... | collective-permute-start | bytes 3538952 | tf_op jit(solution)/shard_map/ppermute | solution.py:31
  30.7 5.4 %collective-permute-start.1 = (bf16[768,768]{1,0:T(8,128)(2,1)S(1)}, bf16[768,768]{1,0:T(8,128)(2,1)S(1)}, u32[]{:S(2)}, u32[]{:S(2)}) collective-permute-start(bf16[768,768]{1,0:T(8,128)(2,1)S(1)} %bitcast.80), channel_id=1, source_target_pairs={{0,8},{8,16},{16,24},{24,32},{32,40},{40,48},{48,56},{56,64},{64,7... | collective-permute-start | bytes 3538952 | tf_op jit(solution)/shard_map/ppermute | solution.py:31
  36.1 1.9 collective-permute-start.2
  38.0 2.4 collective-permute-start.3
  40.4 14.1 %collective-permute-done = bf16[768,768]{1,0:T(8,128)(2,1)S(1)} collective-permute-done((bf16[768,768]{1,0:T(8,128)(2,1)S(1)}, bf16[768,768]{1,0:T(8,128)(2,1)S(1)}, u32[]{:S(2)}, u32[]{:S(2)}) %collective-permute-start) | collective-permute-done | bytes 1179680 | tf_op jit(solution)/shard_map/ppermute | solution.py:31
  55.6 13.4 %collective-permute-done.1 = bf16[768,768]{1,0:T(8,128)(2,1)S(1)} collective-permute-done((bf16[768,768]{1,0:T(8,128)(2,1)S(1)}, bf16[768,768]{1,0:T(8,128)(2,1)S(1)}, u32[]{:S(2)}, u32[]{:S(2)}) %collective-permute-start.1) | collective-permute-done | bytes 1179680 | tf_op jit(solution)/shard_map/ppermute | solution.py:31
  73.6 10.1 %fusion.2 = bf16[5,768,768]{2,0,1:T(8,128)(2,1)} fusion(bf16[5,768,768]{2,1,0:T(8,128)(2,1)} %bitcast_dynamic-update-slice_fusion.5, s32[5]{0:T(128)S(1)} %iota_add_fusion, s32[5]{0:T(128)S(1)} %copy-done), kind=kOutput, calls=%fused_computation.4 | convolution fusion | flops 29491224 | bytes 11796520 | tf_op jit(solution)/shard_map/kd,dij->kij/dot_general | solution.py:67
  83.7 16.7 %bitcast_convert_fusion.1 = bf16[768,768]{1,0:T(8,128)(2,1)S(1)} fusion(bf16[5,768,768]{2,1,0:T(8,128)(2,1)} %param.9, bf16[5,768,768]{2,1,0:T(8,128)(2,1)} %param.8, bf16[5,768,768]{2,0,1:T(8,128)(2,1)} %fusion.2), kind=kOutput, calls=%fused_computation.19 | convolution fusion | flops 9060286464 | bytes 18874368 | tf_op jit(solution)/shard_map/kac,kdc->ad/dot_general | solution.py:74
  100.4 15.4 %all_to_all.21 = bf16[8,96,768]{2,1,0:T(8,128)(2,1)S(1)} all-to-all(bf16[8,96,768]{2,1,0:T(8,128)(2,1)S(1)} %bitcast.89), channel_id=1, replica_groups=mesh['sector'=16,'op'=8] {'op'}, dimensions={0} | all-to-all | bytes 2359296 | tf_op jit(solution)/shard_map/all_to_all | solution.py:41
  116.0 2.6 fusion.20
  118.6 2.4 fusion.36
  121.1 15.1 %all_to_all.22 = bf16[8,96,768]{2,1,0:T(8,128)(2,1)S(1)} all-to-all(bf16[8,96,768]{2,1,0:T(8,128)(2,1)S(1)} %broadcast_in_dim.19), channel_id=1, replica_groups=mesh['sector'=16,'op'=8] {'op'}, dimensions={0} | all-to-all | bytes 2359296 | tf_op jit(solution)/shard_map/all_to_all | solution.py:21
  136.2 2.9 %collective-permute-start.4 = (bf16[768,768]{1,0:T(8,128)(2,1)S(1)}, bf16[768,768]{1,0:T(8,128)(2,1)S(1)}, u32[]{:S(2)}, u32[]{:S(2)}) collective-permute-start(bf16[768,768]{1,0:T(8,128)(2,1)S(1)} %bitcast.84), channel_id=1, source_target_pairs={{0,16},{8,24},{16,32},{24,40},{32,48},{40,56},{48,64},{56,72},{64,... | collective-permute-start | bytes 3538952 | tf_op jit(solution)/shard_map/ppermute | solution.py:31
  139.1 14.6 %collective-permute-start.5 = (bf16[768,768]{1,0:T(8,128)(2,1)S(1)}, bf16[768,768]{1,0:T(8,128)(2,1)S(1)}, u32[]{:S(2)}, u32[]{:S(2)}) collective-permute-start(bf16[768,768]{1,0:T(8,128)(2,1)S(1)} %bitcast.85), channel_id=1, source_target_pairs={{0,8},{8,16},{16,24},{24,32},{32,40},{40,48},{48,56},{56,64},{64,7... | collective-permute-start | bytes 3538952 | tf_op jit(solution)/shard_map/ppermute | solution.py:31
  153.7 1.9 collective-permute-start.6
  155.6 1.9 collective-permute-start.7
  158.7 18.8 %collective-permute-done.5 = bf16[768,768]{1,0:T(8,128)(2,1)S(1)} collective-permute-done((bf16[768,768]{1,0:T(8,128)(2,1)S(1)}, bf16[768,768]{1,0:T(8,128)(2,1)S(1)}, u32[]{:S(2)}, u32[]{:S(2)}) %collective-permute-start.5) | collective-permute-done | bytes 1179680 | tf_op jit(solution)/shard_map/ppermute | solution.py:31
  179.7 2.8 %collective-permute-done.6 = bf16[768,768]{1,0:T(8,128)(2,1)S(1)} collective-permute-done((bf16[768,768]{1,0:T(8,128)(2,1)S(1)}, bf16[768,768]{1,0:T(8,128)(2,1)S(1)}, u32[]{:S(2)}, u32[]{:S(2)}) %collective-permute-start.6) | collective-permute-done | bytes 1179680 | tf_op jit(solution)/shard_map/ppermute | solution.py:31
  186.6 10.1 %fusion = bf16[5,768,768]{2,0,1:T(8,128)(2,1)} fusion(bf16[5,768,768]{2,1,0:T(8,128)(2,1)} %bitcast_dynamic-update-slice_fusion, s32[5]{0:T(128)S(1)} %iota_add_fusion, s32[5]{0:T(128)S(1)} %copy-done), kind=kOutput, calls=%fused_computation.2 | convolution fusion | flops 29491224 | bytes 11796520 | tf_op jit(solution)/shard_map/kd,dij->kij/dot_general | solution.py:67
  196.7 16.5 %bitcast_convert_fusion = bf16[768,768]{1,0:T(8,128)(2,1)S(1)} fusion(bf16[5,768,768]{2,1,0:T(8,128)(2,1)} %param.9, bf16[5,768,768]{2,1,0:T(8,128)(2,1)} %param.8, bf16[5,768,768]{2,0,1:T(8,128)(2,1)} %fusion), kind=kOutput, calls=%fused_computation.18 | convolution fusion | flops 9060286464 | bytes 18874368 | tf_op jit(solution)/shard_map/kac,kdc->ad/dot_general | solution.py:74
  213.2 50.0 %all_to_all.23 = bf16[8,96,768]{2,1,0:T(8,128)(2,1)S(1)} all-to-all(bf16[8,96,768]{2,1,0:T(8,128)(2,1)S(1)} %bitcast.90), channel_id=1, replica_groups=mesh['sector'=16,'op'=8] {'op'}, dimensions={0} | all-to-all | bytes 2359296 | tf_op jit(solution)/shard_map/all_to_all | solution.py:41
  263.4 3.3 %fusion.26 = bf16[1,96,1536]{2,1,0:T(8,128)(2,1)} fusion(bf16[96,768]{1,0:T(8,128)(2,1)S(1)} %reduce_sum.25, bf16[96,1536]{1,0:T(8,128)(2,1)S(1)} %fusion.20, bf16[1,1536,768]{2,1,0:T(8,128)(2,1)} %param.7, pred[1536]{0:T(1024)(128)(4,1)S(1)} %iota_compare_fusion), kind=kOutput, calls=%fused_computation.29 | convolution fusion | flops 228261888 | bytes 3098112 | tf_op jit(solution)/shard_map/ad,ld->al/dot_general | solution.py:80
  (24 shorter events, 13.5 us)
Async XLA Ops:
  27.5 27.1 %collective-permute-start = (bf16[768,768]{1,0:T(8,128)(2,1)S(1)}, bf16[768,768]{1,0:T(8,128)(2,1)S(1)}, u32[]{:S(2)}, u32[]{:S(2)}) collective-permute-start(bf16[768,768]{1,0:T(8,128)(2,1)S(1)} %bitcast.79), channel_id=1, source_target_pairs={{0,16},{8,24},{16,32},{24,40},{32,48},{40,56},{48,64},{56,72},{64,... | collective-permute-start | bytes 3538952 | tf_op jit(solution)/shard_map/ppermute | solution.py:31
  30.7 38.4 %collective-permute-start.1 = (bf16[768,768]{1,0:T(8,128)(2,1)S(1)}, bf16[768,768]{1,0:T(8,128)(2,1)S(1)}, u32[]{:S(2)}, u32[]{:S(2)}) collective-permute-start(bf16[768,768]{1,0:T(8,128)(2,1)S(1)} %bitcast.80), channel_id=1, source_target_pairs={{0,8},{8,16},{16,24},{24,32},{32,40},{40,48},{48,56},{56,64},{64,7... | collective-permute-start | bytes 3538952 | tf_op jit(solution)/shard_map/ppermute | solution.py:31
  36.1 35.2 %collective-permute-start.2 = (bf16[768,768]{1,0:T(8,128)(2,1)S(1)}, bf16[768,768]{1,0:T(8,128)(2,1)S(1)}, u32[]{:S(2)}, u32[]{:S(2)}) collective-permute-start(bf16[768,768]{1,0:T(8,128)(2,1)S(1)} %bitcast.81), channel_id=1, source_target_pairs={{8,0},{16,8},{24,16},{32,24},{40,32},{48,40},{56,48},{64,56},{72,6... | collective-permute-start | bytes 3538952 | tf_op jit(solution)/shard_map/ppermute | solution.py:31
  38.0 34.4 %collective-permute-start.3 = (bf16[768,768]{1,0:T(8,128)(2,1)S(1)}, bf16[768,768]{1,0:T(8,128)(2,1)S(1)}, u32[]{:S(2)}, u32[]{:S(2)}) collective-permute-start(bf16[768,768]{1,0:T(8,128)(2,1)S(1)} %bitcast.82), channel_id=1, source_target_pairs={{16,0},{24,8},{32,16},{40,24},{48,32},{56,40},{64,48},{72,56},{80,... | collective-permute-start | bytes 3538952 | tf_op jit(solution)/shard_map/ppermute | solution.py:31
  40.4 33.2 %copy-start = (s32[5]{0:T(128)S(1)}, s32[5]{0:T(128)}, u32[]{:S(2)}) copy-start(s32[5]{0:T(128)} %param.10) | copy-start | bytes 64
  83.7 32.3 %copy-start.1 = (bf16[1,96,1536]{2,1,0:T(8,128)(2,1)S(1)}, bf16[1,96,1536]{2,1,0:T(8,128)(2,1)}, u32[]{:S(2)}) copy-start(bf16[1,96,1536]{2,1,0:T(8,128)(2,1)} %param.6) | copy-start | bytes 884740
  136.2 21.4 %collective-permute-start.4 = (bf16[768,768]{1,0:T(8,128)(2,1)S(1)}, bf16[768,768]{1,0:T(8,128)(2,1)S(1)}, u32[]{:S(2)}, u32[]{:S(2)}) collective-permute-start(bf16[768,768]{1,0:T(8,128)(2,1)S(1)} %bitcast.84), channel_id=1, source_target_pairs={{0,16},{8,24},{16,32},{24,40},{32,48},{40,56},{48,64},{56,72},{64,... | collective-permute-start | bytes 3538952 | tf_op jit(solution)/shard_map/ppermute | solution.py:31
  139.1 38.4 %collective-permute-start.5 = (bf16[768,768]{1,0:T(8,128)(2,1)S(1)}, bf16[768,768]{1,0:T(8,128)(2,1)S(1)}, u32[]{:S(2)}, u32[]{:S(2)}) collective-permute-start(bf16[768,768]{1,0:T(8,128)(2,1)S(1)} %bitcast.85), channel_id=1, source_target_pairs={{0,8},{8,16},{16,24},{24,32},{32,40},{40,48},{48,56},{56,64},{64,7... | collective-permute-start | bytes 3538952 | tf_op jit(solution)/shard_map/ppermute | solution.py:31
  153.7 28.8 %collective-permute-start.6 = (bf16[768,768]{1,0:T(8,128)(2,1)S(1)}, bf16[768,768]{1,0:T(8,128)(2,1)S(1)}, u32[]{:S(2)}, u32[]{:S(2)}) collective-permute-start(bf16[768,768]{1,0:T(8,128)(2,1)S(1)} %bitcast.86), channel_id=1, source_target_pairs={{8,0},{16,8},{24,16},{32,24},{40,32},{48,40},{56,48},{64,56},{72,6... | collective-permute-start | bytes 3538952 | tf_op jit(solution)/shard_map/ppermute | solution.py:31
  155.6 29.9 %collective-permute-start.7 = (bf16[768,768]{1,0:T(8,128)(2,1)S(1)}, bf16[768,768]{1,0:T(8,128)(2,1)S(1)}, u32[]{:S(2)}, u32[]{:S(2)}) collective-permute-start(bf16[768,768]{1,0:T(8,128)(2,1)S(1)} %bitcast.87), channel_id=1, source_target_pairs={{16,0},{24,8},{32,16},{40,24},{48,32},{56,40},{64,48},{72,56},{80,... | collective-permute-start | bytes 3538952 | tf_op jit(solution)/shard_map/ppermute | solution.py:31
where the time goes:
time: 270 us; the launch traced here: 267 us
  blocking collectives  105 us (39%)
  matrix products  64.2 us (24%)
  waiting for transfers between devices  51 us (19%)
  starting transfers between devices  34.3 us (13%)
  local copies, waits for them, and re-layouts  11.3 us (4%)
    all_to_all x2, blocking collectives, summed_on_arrival(): lax.all_to_all(parts, axis, split_axis=0, concat_axis=0, tiled=True)  65.4 us
    ppermute x8, waiting for transfers between devices, from_behind(): return lax.ppermute(array, axis, pairs)  51 us
    all_to_all x2, blocking collectives, sent_to_all(): return lax.all_to_all(copies, axis, split_axis=0, concat_axis=0, tiled=True)  39.4 us
    ppermute x8, starting transfers between devices, from_behind(): return lax.ppermute(array, axis, pairs)  34.3 us
    dot_general x2, matrix products, on_device(): jnp.einsum('kac,kdc->ad', half_product, right_ops, preferred_element_type...  33.2 us
    dot_general x2, matrix products, on_device(): jnp.einsum('kd,dij->kij', picker, candidates, preferred_element_type=jnp....  20.2 us
    unnamed x12, local copies, waits for them, and re-layouts  8.94 us
    dot_general x2, matrix products, on_device(): jnp.einsum('ad,ld->al', overall_tile_count, masked_basis, preferred_eleme...  5.94 us
  transfers between devices with their start and end apart: 8, of which 5 were waited for; matrix products, arithmetic and copies ran while one was open for 3% of the time, Pallas kernels for 0%

commit v1 on v0

v1 whole, which is shorter than its diff:
```python
import functools

import jax
import jax.numpy as jnp
from jax import lax
from jax.experimental import pallas as pl
from jax.experimental.pallas import tpu as pltpu
from jax.sharding import PartitionSpec as P

BOND = 768
LEFT = 1536
REACH = 2
STEPS = 2
PER = 5
ROWS = 96
CW = 256
CHUNKS = BOND // CW
OPS = 8
increment_width = 0.75
MESH = pl.DeviceIdType.MESH
METHOD = ("B", "B", "N")
ORDER = (0, 2, 1)


def dot_nt(a, b):
    return lax.dot_general(
        a, b, (((1,), (1,)), ((), ())), preferred_element_type=jnp.float32
    )


def dot_nn(a, b):
    return jnp.dot(a, b, preferred_element_type=jnp.float32)


class Names:
    def __init__(self):
        self.index = {}

    def __call__(self, *key):
        return self.index.setdefault(key, len(self.index))


SEMS = 80


def kernel(
    off_ref, size_ref, wf_hbm, basis_hbm, left_hbm, right_hbm, out_ref,
    left, right, basis, cur, x00, x01, x02, x10, x11, x12,
    h, acc, part, arrived, send_sem, recv_sem, rs_send, rs_recv, load_sem,
):
    s = lax.axis_index("sector")
    o = lax.axis_index("op")
    x, zh = o // 2, lax.rem(o, 2)
    core = lax.rem(s, 2)
    chip = s // 2
    has_lo, has_hi = chip > 0, chip < 7
    partner = s + 1 - 2 * core
    z_peer = x * 2 + (1 - zh)
    x_right = lax.rem(x + 1, 4)
    x_left = lax.rem(x + 3, 4)
    x_far = lax.rem(x + 2, 4)
    op_right, op_left = x_right * 2 + zh, x_left * 2 + zh

    loads = {}

    def load(name, src, dst, i):
        cp = pltpu.make_async_copy(src, dst, load_sem.at[i])
        cp.start()
        loads[name] = cp

    load("wf", wf_hbm.at[0], cur, 0)
    load("basis", basis_hbm.at[0], basis, 1)

    barrier = pltpu.get_barrier_semaphore()
    for j in range(1, OPS):
        pl.semaphore_signal(
            barrier, inc=1, device_id={"sector": s, "op": lax.rem(o + j, OPS)}, device_id_type=MESH
        )
    pl.semaphore_signal(barrier, inc=1, device_id={"sector": partner, "op": o}, device_id_type=MESH)

    @pl.when(has_lo)
    def _():
        pl.semaphore_signal(barrier, inc=1, device_id={"sector": s - 2, "op": o}, device_id_type=MESH)

    @pl.when(has_hi)
    def _():
        pl.semaphore_signal(barrier, inc=1, device_id={"sector": s + 2, "op": o}, device_id_type=MESH)

    load("left", left_hbm, left, 2)
    load("right", right_hbm, right, 3)

    xg = ((x00, x01, x02), (x10, x11, x12))

    for bufs in xg:
        for buf in bufs:
            @pl.when(jnp.logical_not(has_lo))
            def _():
                buf[0] = jnp.zeros((BOND, CW), jnp.bfloat16)

            @pl.when(jnp.logical_not(has_lo) & (core == 0))
            def _():
                buf[1] = jnp.zeros((BOND, CW), jnp.bfloat16)

            @pl.when(jnp.logical_not(has_hi))
            def _():
                buf[4] = jnp.zeros((BOND, CW), jnp.bfloat16)

            @pl.when(jnp.logical_not(has_hi) & (core == 1))
            def _():
                buf[3] = jnp.zeros((BOND, CW), jnp.bfloat16)

    columns = lax.broadcasted_iota(jnp.int32, (ROWS, LEFT), 1)
    live = columns < size_ref[0]
    loads["wf"].wait()
    cur[...] = jnp.where(live, cur[...], jnp.zeros((ROWS, LEFT), jnp.bfloat16))
    loads["basis"].wait()

    def rows_of(start, count):
        return pl.ds(pl.multiple_of(start, ROWS), count)

    own_rows = rows_of(o * ROWS, ROWS)
    z_rows = rows_of(z_peer * ROWS, ROWS)
    pair_rows = rows_of(x * 192, 192)
    left_pair = rows_of(x_left * 192, 192)
    right_pair = rows_of(x_right * 192, 192)
    far_pair = rows_of(x_far * 192, 192)
    lo_half = lambda px: rows_of(px * 192, ROWS)
    hi_half = lambda px: rows_of(px * 192 + ROWS, ROWS)

    for step in range(STEPS):
        names = Names()
        waits = []
        bufs = xg[step]

        def send(key, src, dst, sector, op, when=None):
            i = names(*key)

            def copy():
                return pltpu.make_async_remote_copy(
                    src_ref=src, dst_ref=dst,
                    send_sem=send_sem.at[step, i], recv_sem=recv_sem.at[step, i],
                    device_id={"sector": sector, "op": op}, device_id_type=MESH,
                )

            if when is None:
                copy().start()
            else:
                @pl.when(when)
                def _():
                    copy().start()
            waits.append((copy, when))

        def arrive(key, dst, when=None):
            i = names(*key)

            def body():
                pltpu.make_async_remote_copy(
                    src_ref=dst, dst_ref=dst,
                    send_sem=send_sem.at[step, i], recv_sem=recv_sem.at[step, i],
                    device_id={"sector": partner, "op": o}, device_id_type=MESH,
                ).wait_recv()

            if when is None:
                body()
            else:
                pl.when(when)(body)

        def slot_when(slot):
            return {0: has_lo, 2: None, 4: has_hi}[slot]

        def send_y(ch, rows, name):
            buf = bufs[ch]
            send((ch, "y-up", name), buf.at[2, rows], buf.at[0, rows], s + 2, o, has_hi)
            send((ch, "y-dn", name), buf.at[2, rows], buf.at[4, rows], s - 2, o, has_lo)

        def arrive_y(ch, rows, name):
            buf = bufs[ch]
            arrive((ch, "y-up", name), buf.at[0, rows], has_lo)
            arrive((ch, "y-dn", name), buf.at[4, rows], has_hi)

        def gather_z(ch, slot):
            buf = bufs[ch]
            send((ch, slot, "z"), buf.at[slot, own_rows], buf.at[slot, own_rows], s, z_peer, slot_when(slot))

        def gather_x(ch, slot):
            buf = bufs[ch]
            arrive((ch, slot, "z"), buf.at[slot, z_rows], slot_when(slot))
            pair = buf.at[slot, pair_rows]
            send((ch, slot, "right"), pair, pair, s, op_right, slot_when(slot))
            send((ch, slot, "left"), pair, pair, s, op_left, slot_when(slot))

        def relay_x(ch, slot):
            buf = bufs[ch]
            arrive((ch, slot, "right"), buf.at[slot, left_pair], slot_when(slot))
            half = buf.at[slot, lo_half(x_left)]
            send((ch, slot, "right2"), half, half, s, op_right, slot_when(slot))
            arrive((ch, slot, "left"), buf.at[slot, right_pair], slot_when(slot))
            half = buf.at[slot, hi_half(x_right)]
            send((ch, slot, "left2"), half, half, s, op_left, slot_when(slot))

        def finish_x(ch, slot):
            buf = bufs[ch]
            arrive((ch, slot, "right2"), buf.at[slot, lo_half(x_far)], slot_when(slot))
            arrive((ch, slot, "left2"), buf.at[slot, hi_half(x_far)], slot_when(slot))

        def own_across(ch):
            buf = bufs[ch]
            send((ch, "own"), buf.at[2], buf.at[1 + 2 * core], partner, o)

        def far_across(ch):
            buf = bufs[ch]
            there = ((core == 0) & has_hi) | ((core == 1) & has_lo)
            send((ch, "far"), buf.at[4 - 4 * core], buf.at[3 - 2 * core], partner, o, there)

        def arrive_across(ch):
            buf = bufs[ch]
            here = ((core == 0) & has_lo) | ((core == 1) & has_hi)
            arrive((ch, "own"), buf.at[3 - 2 * core])
            arrive((ch, "far"), buf.at[1 + 2 * core], here)

        def halves(ch):
            buf = bufs[ch]

            def body(k, carry):
                d = off_ref[k] + REACH
                h[k] = dot_nn(left[k], buf[d]).astype(jnp.bfloat16)
                return carry

            lax.fori_loop(0, PER, body, 0)

        def second(ch, rows):
            total = None
            for k in range(PER):
                term = dot_nt(h[k, rows], right[k, :, ch * CW : (ch + 1) * CW])
                total = term if total is None else total + term
            return total

        def accumulate(ch, first):
            def body(i, carry):
                rows = pl.ds(pl.multiple_of(i * 384, 384), 384)
                if first:
                    acc[rows] = second(ch, rows)
                else:
                    acc[rows] += second(ch, rows)
                return carry

            lax.fori_loop(0, 2, body, 0)

        rotated = dot_nn(cur[...], basis[...]).astype(jnp.bfloat16)
        for ch in range(CHUNKS):
            bufs[ch][2, own_rows] = rotated[:, ch * CW : (ch + 1) * CW]
        if step == 0:
            pl.semaphore_wait(
                barrier, OPS + has_lo.astype(jnp.int32) + has_hi.astype(jnp.int32)
            )

        blocks = [ch for ch in range(CHUNKS) if METHOD[ch] == "B"]
        early = [ch for ch in range(CHUNKS) if METHOD[ch] == "N"]
        for ch in blocks:
            gather_z(ch, 2)
        for ch in early:
            send_y(ch, own_rows, "rows")
            gather_z(ch, 2)
        for ch in blocks:
            gather_x(ch, 2)
            send_y(ch, pair_rows, "pair")
        for ch in early:
            arrive_y(ch, own_rows, "rows")
            gather_z(ch, 0)
            gather_z(ch, 4)
            gather_x(ch, 2)
        for ch in blocks:
            relay_x(ch, 2)
            send_y(ch, left_pair, "left")
            send_y(ch, right_pair, "right")
        for ch in early:
            gather_x(ch, 0)
            gather_x(ch, 4)
            relay_x(ch, 2)
        for ch in blocks:
            finish_x(ch, 2)
            send_y(ch, far_pair, "far")
            own_across(ch)
        for ch in early:
            finish_x(ch, 2)
            own_across(ch)
            relay_x(ch, 0)
            relay_x(ch, 4)

        if step == 0:
            loads["left"].wait()
            loads["right"].wait()

        for n, ch in enumerate(ORDER):
            if METHOD[ch] == "B":
                arrive_y(ch, pair_rows, "pair")
                arrive_y(ch, right_pair, "left")
                arrive_y(ch, left_pair, "right")
                arrive_y(ch, far_pair, "far")
            else:
                finish_x(ch, 0)
                finish_x(ch, 4)
            far_across(ch)
            arrive_across(ch)
            halves(ch)
            if n < CHUNKS - 1:
                accumulate(ch, n == 0)
        last = ORDER[-1]
        rs_waits = []
        for i in range(2):
            half = lax.rem(x // 2 + 1 + i, 2)
            rows = pl.ds(pl.multiple_of(half * 384, 384), 384)
            part[step, rows] = (acc[rows] + second(last, rows)).astype(jnp.bfloat16)
            for j in range(4):
                peer = half * 4 + lax.rem(lax.rem(o, 4) + 3 - j, 4)
                peer_rows = rows_of(peer * ROWS, ROWS)

                def copy(peer=peer, peer_rows=peer_rows):
                    return pltpu.make_async_remote_copy(
                        src_ref=part.at[step, peer_rows], dst_ref=arrived.at[step, o],
                        send_sem=rs_send.at[step, peer], recv_sem=rs_recv.at[step, o],
                        device_id={"sector": s, "op": peer}, device_id_type=MESH,
                    )

                if i == 1 and j == 3:
                    continue
                copy().start()
                rs_waits.append(copy)

        total = part[step, own_rows].astype(jnp.float32)
        for j in range(1, OPS):
            peer = lax.rem(o + j, OPS)
            pltpu.make_async_remote_copy(
                src_ref=arrived.at[step, peer], dst_ref=arrived.at[step, peer],
                send_sem=rs_send.at[step, peer], recv_sem=rs_recv.at[step, peer],
                device_id={"sector": s, "op": peer}, device_id_type=MESH,
            ).wait_recv()
            total = total + arrived[step, peer].astype(jnp.float32)
        summed = total.astype(jnp.bfloat16)
        lifted = dot_nt(summed, basis[...])
        fresh = (cur[...].astype(jnp.float32) - increment_width * lifted).astype(jnp.bfloat16)
        fresh = jnp.where(live, fresh, jnp.zeros_like(fresh))
        if step == STEPS - 1:
            out_ref[0] = fresh
        else:
            cur[...] = fresh
        for copy in rs_waits:
            copy().wait_send()
        for copy, when in waits:
            if when is None:
                copy().wait_send()
            else:
                @pl.when(when)
                def _():
                    copy().wait_send()
        assert len(names.index) <= SEMS


def on_device(wavefunction, basis, left_ops, right_ops, offsets, sector_sizes):
    any_space = pl.BlockSpec(memory_space=pl.ANY)
    smem = pl.BlockSpec(memory_space=pltpu.SMEM)
    block = pltpu.VMEM((2 * REACH + 1, BOND, CW), jnp.bfloat16)
    return pl.pallas_call(
        kernel,
        out_shape=jax.ShapeDtypeStruct((1, ROWS, LEFT), jnp.bfloat16),
        in_specs=[smem, smem, any_space, any_space, any_space, any_space],
        out_specs=pl.BlockSpec(memory_space=pltpu.VMEM),
        scratch_shapes=[
            pltpu.VMEM((PER, BOND, BOND), jnp.bfloat16),
            pltpu.VMEM((PER, BOND, BOND), jnp.bfloat16),
            pltpu.VMEM((LEFT, BOND), jnp.bfloat16),
            pltpu.VMEM((ROWS, LEFT), jnp.bfloat16),
            block, block, block, block, block, block,
            pltpu.VMEM((PER, BOND, CW), jnp.bfloat16),
            pltpu.VMEM((BOND, BOND), jnp.float32),
            pltpu.VMEM((STEPS, BOND, BOND), jnp.bfloat16),
            pltpu.VMEM((STEPS, OPS, ROWS, BOND), jnp.bfloat16),
            pltpu.SemaphoreType.DMA((STEPS, SEMS)),
            pltpu.SemaphoreType.DMA((STEPS, SEMS)),
            pltpu.SemaphoreType.DMA((STEPS, OPS)),
            pltpu.SemaphoreType.DMA((STEPS, OPS)),
            pltpu.SemaphoreType.DMA((4,)),
        ],
        compiler_params=pltpu.CompilerParams(
            collective_id=0, has_side_effects=True, vmem_limit_bytes=62 * 1024 * 1024
        ),
        name="hamiltonian",
    )(offsets, sector_sizes, wavefunction, basis, left_ops, right_ops)


def solution(mesh):
    return jax.shard_map(
        on_device,
        mesh=mesh,
        in_specs=(
            P("sector", "op", None),
            P("sector", None, None),
            P("op", None, None),
            P("op", None, None),
            P("op"),
            P("sector"),
        ),
        out_specs=P("sector", "op", None),
        check_vma=False,
    )
```

time: 270 us -> 147 us (0.54); the launches traced: 267 us -> 147 us
  Pallas kernels: 0 us -> 145 us
  blocking collectives: 105 us -> 0 us
  matrix products: 64.2 us -> 0 us
  waiting for transfers between devices: 51 us -> 0 us
  starting transfers between devices: 34.3 us -> 0 us
  local copies, waits for them, and re-layouts: 11.3 us -> 1.69 us
    pallas_call x0 -> x1, Pallas kernels: none -> 145 us  [on_device(): pl.pallas_call(kernel, out_shape=jax.ShapeDtypeStruct((1, ROWS, LEFT), jn...]
    all_to_all x4 -> x0, blocking collectives: 105 us -> none  [the longest x2 65.4 us: summed_on_arrival(): lax.all_to_all(parts, axis, split_axis=0, concat_axis=0, tiled=True)]
    dot_general x8 -> x0, matrix products: 64.2 us -> none  [the longest x2 33.2 us: on_device(): jnp.einsum('kac,kdc->ad', half_product, right_ops, preferred_element_type...]
    ppermute x8 -> x0, waiting for transfers between devices: 51 us -> none  [from_behind(): return lax.ppermute(array, axis, pairs)]
    ppermute x8 -> x0, starting transfers between devices: 34.3 us -> none  [from_behind(): return lax.ppermute(array, axis, pairs)]
    unnamed x12 -> x1, local copies, waits for them, and re-layouts: 8.94 us -> 1.69 us
  transfers between devices with their start and end apart: 8 -> 0, of which waited for: 5 -> 0; matrix products, arithmetic and copies ran while one was open for 3% -> 0% of each run, Pallas kernels for 0% -> 0%
where the time goes in v1:
time: 147 us
  Pallas kernels  145 us (99%)
  local copies, waits for them, and re-layouts  1.69 us (1%)
    pallas_call x1, Pallas kernels, on_device(): pl.pallas_call(kernel, out_shape=jax.ShapeDtypeStruct((1, ROWS, LEFT), jn...  145 us

profile of v1, /device:TPU:9, one launch (start us, length us, event | category | flops | bytes accessed | tf_op | source)
XLA Modules:
  0.0 147.0 jit_solution(1936703721914193499)
XLA Ops:
  0.7 144.7 %hamiltonian.1 = bf16[1,96,1536]{2,1,0:T(8,128)(2,1)} custom-call(s32[5]{0:T(128)} %off_ref.1, s32[1]{0:T(128)S(6)} %copy.8.size_ref, bf16[1,96,1536]{2,1,0:T(8,128)(2,1)} %wf_hbm.1, bf16[1,1536,768]{2,1,0:T(8,128)(2,1)} %basis_hbm.1, bf16[5,768,768]{2,1,0:T(8,128)(2,1)} %left_hbm.1, bf16[5,768,768]{2,1,0:T(8,128)(2,1)} %right_hbm.1), custom_call_target="tpu_custom_call" | custom-call | tf_op jit(solution)/shard_map/hamiltonian/pallas_call | solution.py:363
  145.3 1.7 %copy.9 = bf16[1,96,1536]{2,1,0:T(8,128)(2,1)} copy(bf16[1,96,1536]{2,1,0:T(8,128)(2,1)} %hamiltonian.1) | data formatting | bytes 589824

commit v2 on v1

--- a/solution.py
+++ b/solution.py
@@ -54,6 +54,8 @@
     core = lax.rem(s, 2)
     chip = s // 2
     has_lo, has_hi = chip > 0, chip < 7
+    cross_lo, cross_hi = chip == 4, chip == 3
+    plain_lo, plain_hi = has_lo & (chip != 4), has_hi & (chip != 3)
     partner = s + 1 - 2 * core
     z_peer = x * 2 + (1 - zh)
     x_right = lax.rem(x + 1, 4)
@@ -91,7 +93,7 @@
 
     xg = ((x00, x01, x02), (x10, x11, x12))
 
-    for bufs in xg:
+    def blank(bufs):
         for buf in bufs:
             @pl.when(jnp.logical_not(has_lo))
             def _():
@@ -168,10 +170,10 @@
         def slot_when(slot):
             return {0: has_lo, 2: None, 4: has_hi}[slot]
 
-        def send_y(ch, rows, name):
-            buf = bufs[ch]
-            send((ch, "y-up", name), buf.at[2, rows], buf.at[0, rows], s + 2, o, has_hi)
-            send((ch, "y-dn", name), buf.at[2, rows], buf.at[4, rows], s - 2, o, has_lo)
+        def send_y(ch, rows, name, up=has_hi, down=has_lo):
+            buf = bufs[ch]
+            send((ch, "y-up", name), buf.at[2, rows], buf.at[0, rows], s + 2, o, up)
+            send((ch, "y-dn", name), buf.at[2, rows], buf.at[4, rows], s - 2, o, down)
 
         def arrive_y(ch, rows, name):
             buf = bufs[ch]
@@ -182,9 +184,11 @@
             buf = bufs[ch]
             send((ch, slot, "z"), buf.at[slot, own_rows], buf.at[slot, own_rows], s, z_peer, slot_when(slot))
 
+        def arrive_z(ch, slot):
+            arrive((ch, slot, "z"), bufs[ch].at[slot, z_rows], slot_when(slot))
+
         def gather_x(ch, slot):
             buf = bufs[ch]
-            arrive((ch, slot, "z"), buf.at[slot, z_rows], slot_when(slot))
             pair = buf.at[slot, pair_rows]
             send((ch, slot, "right"), pair, pair, s, op_right, slot_when(slot))
             send((ch, slot, "left"), pair, pair, s, op_left, slot_when(slot))
@@ -254,38 +258,43 @@
                 barrier, OPS + has_lo.astype(jnp.int32) + has_hi.astype(jnp.int32)
             )
 
-        blocks = [ch for ch in range(CHUNKS) if METHOD[ch] == "B"]
-        early = [ch for ch in range(CHUNKS) if METHOD[ch] == "N"]
-        for ch in blocks:
-            gather_z(ch, 2)
-        for ch in early:
-            send_y(ch, own_rows, "rows")
-            gather_z(ch, 2)
-        for ch in blocks:
-            gather_x(ch, 2)
-            send_y(ch, pair_rows, "pair")
-        for ch in early:
-            arrive_y(ch, own_rows, "rows")
-            gather_z(ch, 0)
-            gather_z(ch, 4)
-            gather_x(ch, 2)
-        for ch in blocks:
-            relay_x(ch, 2)
-            send_y(ch, left_pair, "left")
-            send_y(ch, right_pair, "right")
-        for ch in early:
-            gather_x(ch, 0)
-            gather_x(ch, 4)
-            relay_x(ch, 2)
-        for ch in blocks:
-            finish_x(ch, 2)
-            send_y(ch, far_pair, "far")
-            own_across(ch)
-        for ch in early:
-            finish_x(ch, 2)
-            own_across(ch)
-            relay_x(ch, 0)
-            relay_x(ch, 4)
+        a, b, d = 0, 1, 2
+        gather_z(a, 2)
+        gather_z(d, 2)
+        gather_z(b, 2)
+        if step == 0:
+            blank(xg[0])
+            blank(xg[1])
+        arrive_z(a, 2)
+        gather_x(a, 2)
+        send_y(a, pair_rows, "pair", plain_hi, plain_lo)
+        arrive_z(d, 2)
+        send_y(d, pair_rows, "pair")
+        arrive_z(b, 2)
+        gather_x(b, 2)
+        gather_x(d, 2)
+        relay_x(a, 2)
+        send_y(a, pair_rows, "pair", cross_hi, cross_lo)
+        send_y(a, left_pair, "left")
+        send_y(a, right_pair, "right")
+        arrive_y(d, pair_rows, "pair")
+        gather_x(d, 0)
+        gather_x(d, 4)
+        finish_x(a, 2)
+        send_y(a, far_pair, "far")
+        own_across(a)
+        relay_x(b, 2)
+        send_y(b, pair_rows, "pair")
+        send_y(b, left_pair, "left")
+        send_y(b, right_pair, "right")
+        relay_x(d, 2)
+        finish_x(b, 2)
+        send_y(b, far_pair, "far")
+        own_across(b)
+        finish_x(d, 2)
+        own_across(d)
+        relay_x(d, 0)
+        relay_x(d, 4)
 
         if step == 0:
             loads["left"].wait()
@@ -294,8 +303,8 @@
         for n, ch in enumerate(ORDER):
             if METHOD[ch] == "B":
                 arrive_y(ch, pair_rows, "pair")
-                arrive_y(ch, right_pair, "left")
-                arrive_y(ch, left_pair, "right")
+                arrive_y(ch, left_pair, "left")
+                arrive_y(ch, right_pair, "right")
                 arrive_y(ch, far_pair, "far")
             else:
                 finish_x(ch, 0)

time: 147 us -> 127 us (0.86)
  Pallas kernels: 145 us -> 124 us
    pallas_call x1, Pallas kernels: 145 us -> 124 us  [on_device(): pl.pallas_call(kernel, out_shape=jax.ShapeDtypeStruct((1, ROWS, LEFT), jn...]
where the time goes in v2:
time: 127 us; the launch traced here: 126 us
  Pallas kernels  124 us (98%)
  local copies, waits for them, and re-layouts  1.69 us (1%)
    pallas_call x1, Pallas kernels, on_device(): pl.pallas_call(kernel, out_shape=jax.ShapeDtypeStruct((1, ROWS, LEFT), jn...  124 us

profile of v2, /device:TPU:9, one launch (start us, length us, event | category | flops | bytes accessed | tf_op | source)
XLA Modules:
  0.0 126.5 jit_solution(3231314682891712757)
XLA Ops:
  0.7 124.1 %hamiltonian.1 = bf16[1,96,1536]{2,1,0:T(8,128)(2,1)} custom-call(s32[5]{0:T(128)} %off_ref.1, s32[1]{0:T(128)S(6)} %copy.8.size_ref, bf16[1,96,1536]{2,1,0:T(8,128)(2,1)} %wf_hbm.1, bf16[1,1536,768]{2,1,0:T(8,128)(2,1)} %basis_hbm.1, bf16[5,768,768]{2,1,0:T(8,128)(2,1)} %left_hbm.1, bf16[5,768,768]{2,1,0:T(8,128)(2,1)} %right_hbm.1), custom_call_target="tpu_custom_call" | custom-call | tf_op jit(solution)/shard_map/hamiltonian/pallas_call | solution.py:372
  124.8 1.7 %copy.9 = bf16[1,96,1536]{2,1,0:T(8,128)(2,1)} copy(bf16[1,96,1536]{2,1,0:T(8,128)(2,1)} %hamiltonian.1) | data formatting | bytes 589824

commit v3 on v2

--- a/solution.py
+++ b/solution.py
@@ -89,7 +89,13 @@
         pl.semaphore_signal(barrier, inc=1, device_id={"sector": s + 2, "op": o}, device_id_type=MESH)
 
     load("left", left_hbm, left, 2)
-    load("right", right_hbm, right, 3)
+    for c in range(CHUNKS):
+        for k in range(PER):
+            span = slice(c * CW, (c + 1) * CW)
+            load(
+                ("right", c, k), right_hbm.at[k, :, span], right.at[c, :, k * CW : (k + 1) * CW],
+                3 + c * PER + k,
+            )
 
     xg = ((x00, x01, x02), (x10, x11, x12))
 
@@ -227,28 +233,21 @@
 
             def body(k, carry):
                 d = off_ref[k] + REACH
-                h[k] = dot_nn(left[k], buf[d]).astype(jnp.bfloat16)
+                span = pl.ds(pl.multiple_of(k * CW, CW), CW)
+                h[:, span] = dot_nn(left[k], buf[d]).astype(jnp.bfloat16)
                 return carry
 
-            lax.fori_loop(0, PER, body, 0)
+            lax.fori_loop(0, PER, body, 0, unroll=True)
 
         def second(ch, rows):
-            total = None
-            for k in range(PER):
-                term = dot_nt(h[k, rows], right[k, :, ch * CW : (ch + 1) * CW])
-                total = term if total is None else total + term
-            return total
+            return dot_nt(h[rows], right[ch])
 
         def accumulate(ch, first):
-            def body(i, carry):
-                rows = pl.ds(pl.multiple_of(i * 384, 384), 384)
-                if first:
-                    acc[rows] = second(ch, rows)
-                else:
-                    acc[rows] += second(ch, rows)
-                return carry
-
-            lax.fori_loop(0, 2, body, 0)
+            rows = slice(None)
+            if first:
+                acc[...] = second(ch, rows)
+            else:
+                acc[...] += second(ch, rows)
 
         rotated = dot_nn(cur[...], basis[...]).astype(jnp.bfloat16)
         for ch in range(CHUNKS):
@@ -257,6 +256,17 @@
             pl.semaphore_wait(
                 barrier, OPS + has_lo.astype(jnp.int32) + has_hi.astype(jnp.int32)
             )
+
+        def bring(ch):
+            if METHOD[ch] == "B":
+                arrive_y(ch, pair_rows, "pair")
+                arrive_y(ch, left_pair, "left")
+                arrive_y(ch, right_pair, "right")
+                arrive_y(ch, far_pair, "far")
+            else:
+                finish_x(ch, 0)
+                finish_x(ch, 4)
+            far_across(ch)
 
         a, b, d = 0, 1, 2
         gather_z(a, 2)
@@ -298,30 +308,29 @@
 
         if step == 0:
             loads["left"].wait()
-            loads["right"].wait()
-
-        for n, ch in enumerate(ORDER):
-            if METHOD[ch] == "B":
-                arrive_y(ch, pair_rows, "pair")
-                arrive_y(ch, left_pair, "left")
-                arrive_y(ch, right_pair, "right")
-                arrive_y(ch, far_pair, "far")
-            else:
-                finish_x(ch, 0)
-                finish_x(ch, 4)
-            far_across(ch)
-            arrive_across(ch)
-            halves(ch)
-            if n < CHUNKS - 1:
-                accumulate(ch, n == 0)
+            for c in range(CHUNKS):
+                for k in range(PER):
+                    loads["right", c, k].wait()
+
+        bring(a)
+        arrive_across(a)
+        halves(a)
+        accumulate(a, True)
+        bring(d)
+        arrive_across(d)
+        halves(d)
+        bring(b)
+        accumulate(d, False)
+        arrive_across(b)
+        halves(b)
         last = ORDER[-1]
         rs_waits = []
         for i in range(2):
             half = lax.rem(x // 2 + 1 + i, 2)
             rows = pl.ds(pl.multiple_of(half * 384, 384), 384)
             part[step, rows] = (acc[rows] + second(last, rows)).astype(jnp.bfloat16)
-            for j in range(4):
-                peer = half * 4 + lax.rem(lax.rem(o, 4) + 3 - j, 4)
+            for j in (((1, 3, 2, 0), (1, 3, 2)))[i]:
+                peer = half * 4 + lax.rem(lax.rem(o, 4) + j, 4)
                 peer_rows = rows_of(peer * ROWS, ROWS)
 
                 def copy(peer=peer, peer_rows=peer_rows):
@@ -331,7 +340,7 @@
                         device_id={"sector": s, "op": peer}, device_id_type=MESH,
                     )
 
-                if i == 1 and j == 3:
+                if i == 1 and j == 0:
                     continue
                 copy().start()
                 rs_waits.append(copy)
@@ -376,11 +385,11 @@
         out_specs=pl.BlockSpec(memory_space=pltpu.VMEM),
         scratch_shapes=[
             pltpu.VMEM((PER, BOND, BOND), jnp.bfloat16),
-            pltpu.VMEM((PER, BOND, BOND), jnp.bfloat16),
+            pltpu.VMEM((CHUNKS, BOND, PER * CW), jnp.bfloat16),
             pltpu.VMEM((LEFT, BOND), jnp.bfloat16),
             pltpu.VMEM((ROWS, LEFT), jnp.bfloat16),
             block, block, block, block, block, block,
-            pltpu.VMEM((PER, BOND, CW), jnp.bfloat16),
+            pltpu.VMEM((BOND, PER * CW), jnp.bfloat16),
             pltpu.VMEM((BOND, BOND), jnp.float32),
             pltpu.VMEM((STEPS, BOND, BOND), jnp.bfloat16),
             pltpu.VMEM((STEPS, OPS, ROWS, BOND), jnp.bfloat16),
@@ -388,7 +397,7 @@
             pltpu.SemaphoreType.DMA((STEPS, SEMS)),
             pltpu.SemaphoreType.DMA((STEPS, OPS)),
             pltpu.SemaphoreType.DMA((STEPS, OPS)),
-            pltpu.SemaphoreType.DMA((4,)),
+            pltpu.SemaphoreType.DMA((3 + CHUNKS * PER,)),
         ],
         compiler_params=pltpu.CompilerParams(
             collective_id=0, has_side_effects=True, vmem_limit_bytes=62 * 1024 * 1024

time: 127 us -> 117 us (0.921)
  Pallas kernels: 124 us -> 114 us
    pallas_call x1, Pallas kernels: 124 us -> 114 us  [on_device(): pl.pallas_call(kernel, out_shape=jax.ShapeDtypeStruct((1, ROWS, LEFT), jn...]
where the time goes in v3:
time: 117 us; the launch traced here: 116 us
  Pallas kernels  114 us (97%)
  local copies, waits for them, and re-layouts  1.69 us (1%)
    pallas_call x1, Pallas kernels, on_device(): pl.pallas_call(kernel, out_shape=jax.ShapeDtypeStruct((1, ROWS, LEFT), jn...  114 us

profile of v3, /device:TPU:9, one launch (start us, length us, event | category | flops | bytes accessed | tf_op | source)
XLA Modules:
  0.0 116.3 jit_solution(11013226278870858880)
XLA Ops:
  0.7 113.9 %hamiltonian.1 = bf16[1,96,1536]{2,1,0:T(8,128)(2,1)} custom-call(s32[5]{0:T(128)} %off_ref.1, s32[1]{0:T(128)S(6)} %copy.8.size_ref, bf16[1,96,1536]{2,1,0:T(8,128)(2,1)} %wf_hbm.1, bf16[1,1536,768]{2,1,0:T(8,128)(2,1)} %basis_hbm.1, bf16[5,768,768]{2,1,0:T(8,128)(2,1)} %left_hbm.1, bf16[5,768,768]{2,1,0:T(8,128)(2,1)} %right_hbm.1), custom_call_target="tpu_custom_call" | custom-call | tf_op jit(solution)/shard_map/hamiltonian/pallas_call | solution.py:381
  114.6 1.7 %copy.9 = bf16[1,96,1536]{2,1,0:T(8,128)(2,1)} copy(bf16[1,96,1536]{2,1,0:T(8,128)(2,1)} %hamiltonian.1) | data formatting | bytes 589824

commit v4 on v3

--- a/solution.py
+++ b/solution.py
@@ -46,7 +46,7 @@
 def kernel(
     off_ref, size_ref, wf_hbm, basis_hbm, left_hbm, right_hbm, out_ref,
     left, right, basis, cur, x00, x01, x02, x10, x11, x12,
-    h, acc, part, arrived, send_sem, recv_sem, rs_send, rs_recv, load_sem,
+    h, acc, rotated, gram, summed, part, arrived, send_sem, recv_sem, rs_send, rs_recv, load_sem,
 ):
     s = lax.axis_index("sector")
     o = lax.axis_index("op")
@@ -135,6 +135,11 @@
     lo_half = lambda px: rows_of(px * 192, ROWS)
     hi_half = lambda px: rows_of(px * 192 + ROWS, ROWS)
 
+    def lift(target):
+        lifted = dot_nt(summed[...], basis[...])
+        fresh = cur[...].astype(jnp.float32) - increment_width * lifted
+        target[...] = fresh.astype(jnp.bfloat16)
+
     for step in range(STEPS):
         names = Names()
         waits = []
@@ -249,13 +254,14 @@
             else:
                 acc[...] += second(ch, rows)
 
-        rotated = dot_nn(cur[...], basis[...]).astype(jnp.bfloat16)
-        for ch in range(CHUNKS):
-            bufs[ch][2, own_rows] = rotated[:, ch * CW : (ch + 1) * CW]
-        if step == 0:
-            pl.semaphore_wait(
-                barrier, OPS + has_lo.astype(jnp.int32) + has_hi.astype(jnp.int32)
-            )
+        def rotate(ch):
+            span = slice(ch * CW, (ch + 1) * CW)
+            if step == 0:
+                rows = dot_nn(cur[...], basis[:, span])
+                rotated[:, span] = rows
+            else:
+                rows = rotated[:, span] - increment_width * dot_nn(summed[...], gram[:, span])
+            bufs[ch][2, own_rows] = rows.astype(jnp.bfloat16)
 
         def bring(ch):
             if METHOD[ch] == "B":
@@ -269,8 +275,15 @@
             far_across(ch)
 
         a, b, d = 0, 1, 2
+        rotate(a)
+        if step == 0:
+            pl.semaphore_wait(
+                barrier, OPS + has_lo.astype(jnp.int32) + has_hi.astype(jnp.int32)
+            )
         gather_z(a, 2)
+        rotate(d)
         gather_z(d, 2)
+        rotate(b)
         gather_z(b, 2)
         if step == 0:
             blank(xg[0])
@@ -290,10 +303,10 @@
         arrive_y(d, pair_rows, "pair")
         gather_x(d, 0)
         gather_x(d, 4)
+        relay_x(b, 2)
         finish_x(a, 2)
         send_y(a, far_pair, "far")
         own_across(a)
-        relay_x(b, 2)
         send_y(b, pair_rows, "pair")
         send_y(b, left_pair, "left")
         send_y(b, right_pair, "right")
@@ -345,6 +358,17 @@
                 copy().start()
                 rs_waits.append(copy)
 
+        if step == 0:
+            basis[...] = jnp.where(
+                lax.broadcasted_iota(jnp.int32, (LEFT, BOND), 0) < size_ref[0],
+                basis[...], jnp.zeros((LEFT, BOND), jnp.bfloat16),
+            )
+            gram[...] = lax.dot_general(
+                basis[...], basis[...], (((0,), (0,)), ((), ())),
+                preferred_element_type=jnp.float32,
+            ).astype(jnp.bfloat16)
+        else:
+            lift(cur)
         total = part[step, own_rows].astype(jnp.float32)
         for j in range(1, OPS):
             peer = lax.rem(o + j, OPS)
@@ -354,14 +378,9 @@
                 device_id={"sector": s, "op": peer}, device_id_type=MESH,
             ).wait_recv()
             total = total + arrived[step, peer].astype(jnp.float32)
-        summed = total.astype(jnp.bfloat16)
-        lifted = dot_nt(summed, basis[...])
-        fresh = (cur[...].astype(jnp.float32) - increment_width * lifted).astype(jnp.bfloat16)
-        fresh = jnp.where(live, fresh, jnp.zeros_like(fresh))
+        summed[...] = total.astype(jnp.bfloat16)
         if step == STEPS - 1:
-            out_ref[0] = fresh
-        else:
-            cur[...] = fresh
+            lift(out_ref.at[0])
         for copy in rs_waits:
             copy().wait_send()
         for copy, when in waits:
@@ -391,6 +410,9 @@
             block, block, block, block, block, block,
             pltpu.VMEM((BOND, PER * CW), jnp.bfloat16),
             pltpu.VMEM((BOND, BOND), jnp.float32),
+            pltpu.VMEM((ROWS, BOND), jnp.float32),
+            pltpu.VMEM((BOND, BOND), jnp.bfloat16),
+            pltpu.VMEM((ROWS, BOND), jnp.bfloat16),
             pltpu.VMEM((STEPS, BOND, BOND), jnp.bfloat16),
             pltpu.VMEM((STEPS, OPS, ROWS, BOND), jnp.bfloat16),
             pltpu.SemaphoreType.DMA((STEPS, SEMS)),

time: 117 us -> 115 us (0.983)
    pallas_call x1, Pallas kernels: 114 us -> 113 us  [on_device(): pl.pallas_call(kernel, out_shape=jax.ShapeDtypeStruct((1, ROWS, LEFT), jn...]
where the time goes in v4:
time: 115 us
  Pallas kernels  113 us (98%)
  local copies, waits for them, and re-layouts  1.69 us (1%)
    pallas_call x1, Pallas kernels, on_device(): pl.pallas_call(kernel, out_shape=jax.ShapeDtypeStruct((1, ROWS, LEFT), jn...  113 us

profile of v4, /device:TPU:9, one launch (start us, length us, event | category | flops | bytes accessed | tf_op | source)
XLA Modules:
  0.0 114.9 jit_solution(5265909051469403603)
XLA Ops:
  0.7 112.5 %hamiltonian.1 = bf16[1,96,1536]{2,1,0:T(8,128)(2,1)} custom-call(s32[5]{0:T(128)} %off_ref.1, s32[1]{0:T(128)S(6)} %copy.8.size_ref, bf16[1,96,1536]{2,1,0:T(8,128)(2,1)} %wf_hbm.1, bf16[1,1536,768]{2,1,0:T(8,128)(2,1)} %basis_hbm.1, bf16[5,768,768]{2,1,0:T(8,128)(2,1)} %left_hbm.1, bf16[5,768,768]{2,1,0:T(8,128)(2,1)} %right_hbm.1), custom_call_target="tpu_custom_call" | custom-call | tf_op jit(solution)/shard_map/hamiltonian/pallas_call | solution.py:400
  113.2 1.7 %copy.9 = bf16[1,96,1536]{2,1,0:T(8,128)(2,1)} copy(bf16[1,96,1536]{2,1,0:T(8,128)(2,1)} %hamiltonian.1) | data formatting | bytes 589824

commit v5 on v4

--- a/solution.py
+++ b/solution.py
@@ -342,7 +342,7 @@
             half = lax.rem(x // 2 + 1 + i, 2)
             rows = pl.ds(pl.multiple_of(half * 384, 384), 384)
             part[step, rows] = (acc[rows] + second(last, rows)).astype(jnp.bfloat16)
-            for j in (((1, 3, 2, 0), (1, 3, 2)))[i]:
+            for j in (((1, 3, 0, 2), (1, 3, 2)))[i]:
                 peer = half * 4 + lax.rem(lax.rem(o, 4) + j, 4)
                 peer_rows = rows_of(peer * ROWS, ROWS)
 

time: 115 us -> 115 us (level)
  no operation moved by 1% of the time
where the time goes in v5:
time: 115 us
  Pallas kernels  113 us (98%)
  local copies, waits for them, and re-layouts  1.69 us (1%)
    pallas_call x1, Pallas kernels, on_device(): pl.pallas_call(kernel, out_shape=jax.ShapeDtypeStruct((1, ROWS, LEFT), jn...  113 us

profile of v5, /device:TPU:9, one launch (start us, length us, event | category | flops | bytes accessed | tf_op | source)
XLA Modules:
  0.0 114.9 jit_solution(13267194209787689522)
XLA Ops:
  0.7 112.5 %hamiltonian.1 = bf16[1,96,1536]{2,1,0:T(8,128)(2,1)} custom-call(s32[5]{0:T(128)} %off_ref.1, s32[1]{0:T(128)S(6)} %copy.8.size_ref, bf16[1,96,1536]{2,1,0:T(8,128)(2,1)} %wf_hbm.1, bf16[1,1536,768]{2,1,0:T(8,128)(2,1)} %basis_hbm.1, bf16[5,768,768]{2,1,0:T(8,128)(2,1)} %left_hbm.1, bf16[5,768,768]{2,1,0:T(8,128)(2,1)} %right_hbm.1), custom_call_target="tpu_custom_call" | custom-call | tf_op jit(solution)/shard_map/hamiltonian/pallas_call | solution.py:400
  113.2 1.7 %copy.9 = bf16[1,96,1536]{2,1,0:T(8,128)(2,1)} copy(bf16[1,96,1536]{2,1,0:T(8,128)(2,1)} %hamiltonian.1) | data formatting | bytes 589824
